TPU v7x, 256 devices: a whole 4x4x8 slice. The times are simulated.
256 devices in a mesh: expert: 32 (over z_hi, y, core), dp: 8 (over z_lo, x).
Axes of the slice: x: 4, y: 4, z: 8 (z_hi: 4, z_lo: 2; z = z_hi * 2 + z_lo), core: 2. Of those that a mesh axis runs over, the one named last changes fastest.
Arguments:
- tokens: bfloat16 [32768, 4096], P(('expert', 'dp')), may hold values from -6 to 6
- route: int32 [32768, 2], P(('expert', 'dp')), may hold values from 0 to 63, all different within a row; in each aligned block of 128 rows (0 to 127, 128 to 255, ...) at most 12 rows name the same one
- gate_output_gradient: bfloat16 [32768, 2, 1536], P(('expert', 'dp')), may hold values from -0.4375 to 0.4375
- frozen_gate_weight: bfloat16 [64, 4096, 1536], P('expert', 'dp'), may hold values from -0.09375 to 0.09375
- adapter_first: bfloat16 [64, 4096, 16], P('expert'), may hold values from -0.09375 to 0.09375
- adapter_second: bfloat16 [64, 16, 1536], P('expert'), may hold values from -0.15625 to 0.15625
Outputs:
- grad_a: float32 [64, 4096, 16], P('expert')
- grad_b: float32 [64, 16, 1536], P('expert')
Inputs may be any that keep to these rules, and one draw needn't show every extreme that they name: `route`: each row names 2 different experts. Within each device's aligned block of 128 rows no expert is named more than 12 times.
All inputs are finite; a program needn't handle non-finite values.
Results may differ from a plain program's by a relative error of at most 0.0043.
Values may be sent and summed in bfloat16 or wider, within the bound.
No kernel may reach another device: no remote copies, remote signals or barrier semaphores. Data moves between devices by JAX's collectives and lax.ppermute only.
A program may use at most 128 MiB of HBM per device.

v0:
```python
import jax
import jax.numpy as jnp
from jax import lax
from jax.sharding import PartitionSpec as P

ADAPTER_SCALE = 2.0


def silu_slope(gate_preactivation):
    squash = jax.nn.sigmoid(gate_preactivation)
    return squash * (1.0 + gate_preactivation * (1.0 - squash))


def block_product(input_rows, piece):
    return jnp.dot(input_rows, piece, preferred_element_type=jnp.float32)


def prepare(input_rows, rows_g):
    block = 128
    return (input_rows, rows_g, None, block)


def adapter_grads(input_rows, rows_g, frozen_output, first_adapter_factor, second_adapter_factor):
    rank_reduced_output = jnp.dot(
        input_rows, first_adapter_factor, preferred_element_type=jnp.float32
    ).astype(jnp.bfloat16)
    gate_preactivation = frozen_output + ADAPTER_SCALE * jnp.dot(
        rank_reduced_output, second_adapter_factor, preferred_element_type=jnp.float32
    )
    activation_slope = (rows_g.astype(jnp.float32) * silu_slope(gate_preactivation)).astype(
        jnp.bfloat16
    )
    up_gradient = ADAPTER_SCALE * jnp.einsum(
        "nr,nf->rf", rank_reduced_output, activation_slope, preferred_element_type=jnp.float32
    )
    rank_backward = jnp.einsum(
        "nf,rf->nr", activation_slope, second_adapter_factor, preferred_element_type=jnp.float32
    ).astype(jnp.bfloat16)
    down_gradient = ADAPTER_SCALE * jnp.einsum(
        "nd,nr->dr", input_rows, rank_backward, preferred_element_type=jnp.float32
    )
    return (down_gradient, up_gradient)


def local(tokens, route, gate_output_gradient, frozen_gate_weight, adapter_first, adapter_second):
    experts_here = frozen_gate_weight.shape[0]
    columns = lax.axis_size("expert")
    experts = experts_here * columns
    tok_rows = tokens.shape[0]
    top_count = route.shape[1]
    width = tokens.shape[1]
    hidden = gate_output_gradient.shape[2]
    capacity = 3 * tok_rows * top_count // experts
    slot_count = tok_rows * top_count
    flat_route = route.reshape(slot_count)
    labels = jnp.arange(experts, dtype=jnp.int32)
    one_hot = (flat_route[:, None] == labels[None, :]).astype(jnp.int32)
    ranks = jnp.sum((jnp.cumsum(one_hot, axis=0) - one_hot) * one_hot, axis=1)
    target = (flat_route % experts_here * columns + flat_route // experts_here) * capacity + ranks
    positions = jnp.arange(experts * capacity, dtype=jnp.int32)
    hits = target[None, :] == positions[:, None]
    filled = jnp.any(hits, axis=1)
    slot_ids = jnp.arange(slot_count, dtype=jnp.int32)
    source_slot = jnp.sum(jnp.where(hits, slot_ids[None, :], 0), axis=1)
    send_x = tokens[source_slot // top_count].reshape(experts_here, columns, capacity, width)
    flat_grad = gate_output_gradient.reshape(slot_count, hidden)
    send_g = jnp.where(
        filled[:, None], flat_grad[source_slot], jnp.zeros((), gate_output_gradient.dtype)
    )
    send_g = send_g.reshape(experts_here, columns, capacity, hidden)
    group_rows = columns * capacity
    recv_x, recv_g = (
        lax.all_to_all(send_x, "expert", split_axis=1, concat_axis=1, tiled=True),
        lax.all_to_all(send_g, "expert", split_axis=1, concat_axis=1, tiled=True),
    )
    input_rows = recv_x.reshape(experts_here, group_rows, width)
    rows_g = recv_g.reshape(experts_here, group_rows, hidden)
    ready_inputs = [
        prepare(input_rows[local_result], rows_g[local_result])
        for local_result in range(experts_here)
    ]

    def add_rows(piece):
        return jnp.stack(
            [
                block_product(ready_inputs[local_result][0], piece[local_result])
                for local_result in range(experts_here)
            ]
        )

    frozen_output = add_rows(lax.all_gather(frozen_gate_weight, "dp", axis=1, tiled=True))
    results = [
        adapter_grads(
            ready_inputs[local_result][0],
            ready_inputs[local_result][1],
            frozen_output[local_result],
            adapter_first[local_result],
            adapter_second[local_result],
        )
        for local_result in range(experts_here)
    ]
    grad_a_local = jnp.stack([result[0] for result in results])
    grad_b_local = jnp.stack([result[1] for result in results])
    grad_a, grad_b = lax.psum((grad_a_local, grad_b_local), "dp")
    return (grad_a, grad_b)


def solution(mesh):
    return jax.shard_map(
        local,
        mesh=mesh,
        in_specs=(
            P(("expert", "dp"), None),
            P(("expert", "dp"), None),
            P(("expert", "dp"), None, None),
            P("expert", "dp", None),
            P("expert", None, None),
            P("expert", None, None),
        ),
        out_specs=(P("expert", None, None), P("expert", None, None)),
        check_vma=False,
    )
```

profile of v0, /device:TPU:8, one launch (start us, length us, event | category | flops | bytes accessed | tf_op | source)
XLA Modules:
  0.0 568.3 jit_solution(11198235258273988007)
XLA Ops:
  7.2 0.7 all-gather.2.cloned.1.call-update
  9.9 3.9 gather_fusion.1
  13.7 4.8 gather.10
  18.8 2.2 broadcast_select_fusion
  21.0 3.8 copy.20
  24.8 11.7 %all-to-all-start.1 = ((bf16[2,32,12,1536]{3,0,2,1:T(2,128)(2,1)}), bf16[2,32,12,1536]{3,0,2,1:T(2,128)(2,1)S(1)}, u32[]{:S(2)}, u32[]{:S(2)}) async-start(bf16[2,32,12,1536]{3,0,2,1:T(2,128)(2,1)} %copy.20), calls=%async_computation.1 | async-start | bytes 4718592 | tf_op jit(solution)/shard_map/all_to_all | solution.py:74
  36.6 5.7 gather_fusion
  42.2 9.8 %reshape.176 = bf16[2,32,12,4096]{3,2,1,0:T(8,128)(2,1)} reshape(bf16[768,4096]{1,0:T(8,128)(2,1)} %gather_fusion) | data formatting | bytes 12582912 | tf_op jit(solution)/shard_map/reshape | solution.py:65
  52.0 13.6 %copy.19 = bf16[2,32,12,4096]{3,0,2,1:T(2,128)(2,1)} copy(bf16[2,32,12,4096]{3,2,1,0:T(8,128)(2,1)} %reshape.176) | data formatting | bytes 12582912 | tf_op jit(solution)/shard_map/reshape | solution.py:65
  65.5 53.0 %all-to-all-done.1 = bf16[2,32,12,1536]{3,0,2,1:T(2,128)(2,1)S(1)} async-done(((bf16[2,32,12,1536]{3,0,2,1:T(2,128)(2,1)}), bf16[2,32,12,1536]{3,0,2,1:T(2,128)(2,1)S(1)}, u32[]{:S(2)}, u32[]{:S(2)}) %all-to-all-start.1) | async-done | bytes 2359328 | tf_op jit(solution)/shard_map/all_to_all | solution.py:74
  118.6 5.3 all-to-all-start
  124.0 15.2 %fusion.7 = (f32[32,12,1536]{2,1,0:T(8,128)}, f32[32,12,1536]{2,1,0:T(8,128)}) fusion(bf16[2,32,12,1536]{3,0,2,1:T(2,128)(2,1)S(1)} %all-to-all-done.1), kind=kLoop, calls=%fused_computation.20 | loop fusion | flops 1179648 | bytes 7077888 | tf_op jit(solution)/shard_map/convert_element_type | solution.py:30
  139.1 3.6 reshape.178
  142.7 3.6 reshape.179
  146.2 186.4 %all-to-all-done = bf16[2,32,12,4096]{3,0,2,1:T(2,128)(2,1)} async-done(((bf16[2,32,12,4096]{3,0,2,1:T(2,128)(2,1)}), bf16[2,32,12,4096]{3,0,2,1:T(2,128)(2,1)}, u32[]{:S(2)}, u32[]{:S(2)}) %all-to-all-start) | async-done | bytes 6291488 | tf_op jit(solution)/shard_map/all_to_all | solution.py:73
  332.6 33.0 %slice_reduce_fusion.1 = (bf16[32,12,4096]{2,1,0:T(8,128)(2,1)}, bf16[32,12,4096]{2,1,0:T(8,128)(2,1)}) fusion(bf16[2,32,12,4096]{3,0,2,1:T(2,128)(2,1)} %all-to-all-done), kind=kLoop, calls=%fused_computation.7 | loop fusion | bytes 12582912 | tf_op jit(solution)/shard_map/slice | solution.py:79
  365.6 5.6 squeeze.26
  371.2 5.6 squeeze.30
  376.8 3.0 convolution_convert_fusion.3
  379.8 0.9 convolution_convert_fusion.1
  380.8 69.1 %all-gather.2.cloned.1.call-done = bf16[2,4096,1536]{2,1,0:T(8,128)(2,1)} async-done(((bf16[2,512,1536]{2,1,0:T(8,128)(2,1)}), bf16[2,4096,1536]{2,1,0:T(8,128)(2,1)}) %all-gather.2.cloned.1.call-update) | async-done | bytes 25165840 | tf_op jit(solution)/shard_map/all_gather | solution.py:91
  449.8 9.3 %fusion.1 = f32[384,1536]{1,0:T(8,128)S(1)} fusion(bf16[384,4096]{1,0:T(8,128)(2,1)} %squeeze.26, bf16[2,4096,1536]{2,1,0:T(8,128)(2,1)} %all-gather.2.cloned.1.call-done), kind=kOutput, calls=%fused_computation.5 | convolution fusion | flops 4831838208 | bytes 18087936 | tf_op jit(solution)/shard_map/dot_general | solution.py:15
  459.2 1.1 multiply_convert_fusion.1
  460.6 3.0 fusion.3
  463.6 9.1 %fusion = f32[384,1536]{1,0:T(8,128)S(1)} fusion(bf16[384,4096]{1,0:T(8,128)(2,1)} %squeeze.30, bf16[2,4096,1536]{2,1,0:T(8,128)(2,1)} %all-gather.2.cloned.1.call-done), kind=kOutput, calls=%fused_computation.3 | convolution fusion | flops 4831838208 | bytes 18087936 | tf_op jit(solution)/shard_map/dot_general | solution.py:15
  472.7 1.1 multiply_convert_fusion
  474.1 3.1 fusion.2
  477.2 0.7 pad_maximum_fusion.1
  477.9 0.8 pad_maximum_fusion
  478.7 79.3 %all-reduce.3.cloned.1.call-done = (f32[2,4096,16]{1,2,0:T(8,128)}, f32[2,16,1536]{2,1,0:T(8,128)}) async-done(((f32[2,4096,16]{1,2,0:T(8,128)}, f32[2,16,1536]{2,1,0:T(8,128)}), (f32[2,4096,16]{1,2,0:T(8,128)}, f32[2,16,1536]{2,1,0:T(8,128)})) %all-reduce.3.cloned.1.call-update) | async-done | bytes 720912 | tf_op jit(solution)/shard_map/psum | solution.py:104
  558.0 1.9 copy.29
  559.9 1.6 copy.30
  (39 shorter events, 2.9 us)
Async XLA Ops:
  7.2 29.4 %copy-start = (bf16[128,4096]{1,0:T(8,128)(2,1)S(1)}, bf16[128,4096]{1,0:T(8,128)(2,1)}, u32[]{:S(2)}) copy-start(bf16[128,4096]{1,0:T(8,128)(2,1)} %param.6) | copy-start | bytes 3145732
  7.2 0.8 copy-start.8
  7.2 2.0 copy-start.5
  7.2 442.6 %all-gather.2.cloned.1.call-start = ((), (), s32[]{:S(2)}) async-start(), calls=%async_computation.2 | async-start | bytes 28311552 | tf_op jit(solution)/shard_map/all_gather | solution.py:91
  24.8 93.7 %all-to-all-start.1 = ((bf16[2,32,12,1536]{3,0,2,1:T(2,128)(2,1)}), bf16[2,32,12,1536]{3,0,2,1:T(2,128)(2,1)S(1)}, u32[]{:S(2)}, u32[]{:S(2)}) async-start(bf16[2,32,12,1536]{3,0,2,1:T(2,128)(2,1)} %copy.20), calls=%async_computation.1 | async-start | bytes 4718592 | tf_op jit(solution)/shard_map/all_to_all | solution.py:74
  118.6 214.0 %all-to-all-start = ((bf16[2,32,12,4096]{3,0,2,1:T(2,128)(2,1)}), bf16[2,32,12,4096]{3,0,2,1:T(2,128)(2,1)}, u32[]{:S(2)}, u32[]{:S(2)}) async-start(bf16[2,32,12,4096]{3,0,2,1:T(2,128)(2,1)} %copy.19), calls=%async_computation | async-start | bytes 12582912 | tf_op jit(solution)/shard_map/all_to_all | solution.py:73
  123.9 434.1 %all-reduce.3.cloned.1.call-start = ((), (), s32[]{:S(2)}) async-start(), calls=%async_computation.3 | async-start | bytes 1441792 | tf_op jit(solution)/shard_map/psum | solution.py:104
  371.2 5.6 copy-start.6
  376.8 3.0 copy-start.2
  380.8 78.4 %copy-start.7 = (bf16[2,16,1536]{2,1,0:T(8,128)(2,1)S(1)}, bf16[2,16,1536]{2,1,0:T(8,128)(2,1)}, u32[]{:S(2)}) copy-start(bf16[2,16,1536]{2,1,0:T(8,128)(2,1)} %param.11) | copy-start | bytes 294916
  449.8 9.3 %copy-start.4 = (f32[384,1536]{1,0:T(8,128)S(1)}, f32[384,1536]{1,0:T(8,128)}, u32[]{:S(2)}) copy-start(f32[384,1536]{1,0:T(8,128)} %reshape.178) | copy-start | bytes 7077892
  463.6 9.1 %copy-start.3 = (f32[384,1536]{1,0:T(8,128)S(1)}, f32[384,1536]{1,0:T(8,128)}, u32[]{:S(2)}) copy-start(f32[384,1536]{1,0:T(8,128)} %reshape.179) | copy-start | bytes 7077892
  474.1 87.4 %copy-start.1 = (bf16[128,4096]{1,0:T(8,128)(2,1)S(1)}, bf16[128,4096]{1,0:T(8,128)(2,1)}, u32[]{:S(2)}) copy-start(bf16[128,4096]{1,0:T(8,128)(2,1)} %param.6) | copy-start | bytes 3145732
Sparse Core Ops, SparseCore 0:
  9.8 439.9 all-gather.1
  478.8 79.1 all-reduce.2
where the time goes:
time: 569 us; the launch traced here: 568 us
  waiting for transfers between devices  388 us (68%)
  local copies, waits for them, and re-layouts  97.3 us (17%)
  matrix products  31.2 us (5%)
  other arithmetic  20 us (4%)
  starting transfers between devices  17.1 us (3%)
  between operations  14.2 us (2%)
    all_to_all x1, waiting for transfers between devices, local(): lax.all_to_all(send_x, 'expert', split_axis=1, concat_axis=1, tiled=True)  186 us
    psum x1, waiting for transfers between devices, local(): grad_a, grad_b = lax.psum((grad_a_local, grad_b_local), 'dp')  79.3 us
    all_gather x1, waiting for transfers between devices, local(): lax.all_gather(frozen_gate_weight, 'dp', axis=1, tiled=True)  69.1 us
    all_to_all x1, waiting for transfers between devices, local(): lax.all_to_all(send_g, 'expert', split_axis=1, concat_axis=1, tiled=True)  53 us
    slice x1, local copies, waits for them, and re-layouts, local(): input_rows[local_result]  33 us
    reshape x2, local copies, waits for them, and re-layouts, local(): tokens[source_slot // top_count]  23.3 us
    dot_general x2, matrix products, block_product(): return jnp.dot(input_rows, piece, preferred_element_type=jnp.float32)  18.4 us
    convert_element_type x1, other arithmetic, adapter_grads(): rows_g.astype(jnp.float32) * silu_slope(gate_preactivation)  15.2 us
  transfers between devices with their start and end apart: 4, of which 4 were waited for; matrix products, arithmetic and copies ran while one was open for 20% of the time, Pallas kernels for 0%

commit v1 on v0

--- a/solution.py
+++ b/solution.py
@@ -4,6 +4,13 @@
 from jax.sharding import PartitionSpec as P
 
 ADAPTER_SCALE = 2.0
+
+
+def pass_slots(vector):
+    front = jnp.concatenate(
+        lax.all_to_all(jnp.stack(lax.axis_size("dp") * [vector], axis=0), "dp", 0, 0), axis=1
+    )
+    return front
 
 
 def silu_slope(gate_preactivation):
@@ -88,7 +95,7 @@
             ]
         )
 
-    frozen_output = add_rows(lax.all_gather(frozen_gate_weight, "dp", axis=1, tiled=True))
+    frozen_output = add_rows(pass_slots(frozen_gate_weight))
     results = [
         adapter_grads(
             ready_inputs[local_result][0],

time: 569 us -> 657 us (1.15)
  blocking collectives: 0 us -> 117 us
  waiting for transfers between devices: 388 us -> 305 us
  starting transfers between devices: 17.1 us -> 50.2 us
  local copies, waits for them, and re-layouts: 97.3 us -> 122 us
    all_to_all x0 -> x1, blocking collectives: none -> 117 us  [local(): lax.all_to_all(send_x, 'expert', split_axis=1, concat_axis=1, tiled=True)]
    all_gather x1 -> x0, waiting for transfers between devices: 69.1 us -> none  [local(): lax.all_gather(frozen_gate_weight, 'dp', axis=1, tiled=True)]
    all_to_all x1, starting transfers between devices: 5.3 us -> 38.2 us  [pass_slots(): lax.all_to_all(jnp.stack(lax.axis_size('dp') * [vector], axis=0), 'dp', 0...]
    all_to_all x1, waiting for transfers between devices: 53 us -> 23.8 us  [local(): lax.all_to_all(send_g, 'expert', split_axis=1, concat_axis=1, tiled=True)]
    all_to_all x1, waiting for transfers between devices: 186 us -> 202 us  [pass_slots(): lax.all_to_all(jnp.stack(lax.axis_size('dp') * [vector], axis=0), 'dp', 0...]
    slice x1 -> x2, local copies, waits for them, and re-layouts: 0.18 us -> 14 us  [the longest x1 13.8 us: add_rows(): piece[local_result]]
    another operation x1 -> x2, local copies, waits for them, and re-layouts: 0.01 us -> 8.61 us  [the longest x1 8.61 us: pass_slots(): jnp.stack(lax.axis_size('dp') * [vector], axis=0)]
  transfers between devices with their start and end apart: 4 -> 3, of which waited for: 4 -> 3; matrix products, arithmetic and copies ran while one was open for 20% -> 15% of each run, Pallas kernels for 0% -> 0%
where the time goes in v1:
time: 657 us; the launch traced here: 656 us
  waiting for transfers between devices  305 us (46%)
  local copies, waits for them, and re-layouts  122 us (19%)
  blocking collectives  117 us (18%)
  starting transfers between devices  50.2 us (8%)
  matrix products  26.9 us (4%)
  other arithmetic  19.9 us (3%)
  between operations  14.2 us (2%)
    all_to_all x1, waiting for transfers between devices, pass_slots(): lax.all_to_all(jnp.stack(lax.axis_size('dp') * [vector], axis=0), 'dp', 0...  202 us
    all_to_all x1, blocking collectives, local(): lax.all_to_all(send_x, 'expert', split_axis=1, concat_axis=1, tiled=True)  117 us
    psum x1, waiting for transfers between devices, local(): grad_a, grad_b = lax.psum((grad_a_local, grad_b_local), 'dp')  78.7 us
    all_to_all x1, starting transfers between devices, pass_slots(): lax.all_to_all(jnp.stack(lax.axis_size('dp') * [vector], axis=0), 'dp', 0...  38.2 us
    slice x1, local copies, waits for them, and re-layouts, local(): input_rows[local_result]  32.9 us
    all_to_all x1, waiting for transfers between devices, local(): lax.all_to_all(send_g, 'expert', split_axis=1, concat_axis=1, tiled=True)  23.8 us
    reshape x2, local copies, waits for them, and re-layouts, local(): tokens[source_slot // top_count]  23.3 us
    convert_element_type x1, other arithmetic, adapter_grads(): rows_g.astype(jnp.float32) * silu_slope(gate_preactivation)  15 us
  transfers between devices with their start and end apart: 3, of which 3 were waited for; matrix products, arithmetic and copies ran while one was open for 15% of the time, Pallas kernels for 0%

profile of v1, /device:TPU:8, one launch (start us, length us, event | category | flops | bytes accessed | tf_op | source)
XLA Modules:
  0.0 655.8 jit_solution(7743102896658114524)
XLA Ops:
  9.9 2.3 reshape.187
  12.2 3.8 gather_fusion.1
  16.0 4.8 gather.10
  20.7 2.2 broadcast_select_fusion
  22.9 3.8 copy.20
  26.7 11.7 %all-to-all-start.1 = ((bf16[2,32,12,1536]{3,0,2,1:T(2,128)(2,1)}), bf16[2,32,12,1536]{3,0,2,1:T(2,128)(2,1)S(1)}, u32[]{:S(2)}, u32[]{:S(2)}) async-start(bf16[2,32,12,1536]{3,0,2,1:T(2,128)(2,1)} %copy.20), calls=%async_computation.1 | async-start | bytes 4718592 | tf_op jit(solution)/shard_map/all_to_all | solution.py:81
  38.4 5.8 gather_fusion
  44.2 9.8 %reshape.186 = bf16[2,32,12,4096]{3,2,1,0:T(8,128)(2,1)} reshape(bf16[768,4096]{1,0:T(8,128)(2,1)} %gather_fusion) | data formatting | bytes 12582912 | tf_op jit(solution)/shard_map/reshape | solution.py:72
  54.0 13.6 %copy.19 = bf16[2,32,12,4096]{3,0,2,1:T(2,128)(2,1)} copy(bf16[2,32,12,4096]{3,2,1,0:T(8,128)(2,1)} %reshape.186) | data formatting | bytes 12582912 | tf_op jit(solution)/shard_map/reshape | solution.py:72
  67.6 23.8 %all-to-all-done.1 = bf16[2,32,12,1536]{3,0,2,1:T(2,128)(2,1)S(1)} async-done(((bf16[2,32,12,1536]{3,0,2,1:T(2,128)(2,1)}), bf16[2,32,12,1536]{3,0,2,1:T(2,128)(2,1)S(1)}, u32[]{:S(2)}, u32[]{:S(2)}) %all-to-all-start.1) | async-done | bytes 2359328 | tf_op jit(solution)/shard_map/all_to_all | solution.py:81
  91.4 117.3 %all_to_all.15 = bf16[2,32,12,4096]{3,0,2,1:T(2,128)(2,1)} all-to-all(bf16[2,32,12,4096]{3,0,2,1:T(2,128)(2,1)} %copy.19), channel_id=1, replica_groups=mesh['expert'=32,'dp'=8] {'expert'}, dimensions={1} | all-to-all | bytes 12582912 | tf_op jit(solution)/shard_map/all_to_all | solution.py:80
  208.7 8.6 %stack.14 = bf16[8,2,512,1536]{3,2,1,0:T(8,128)(2,1)} broadcast(bf16[2,512,1536]{2,1,0:T(8,128)(2,1)S(1)} %copy-done.4), dimensions={1,2,3} | broadcast | bytes 28311552 | tf_op jit(solution)/shard_map/stack | solution.py:11
  217.3 38.2 %all-to-all-start.2 = ((bf16[8,2,512,1536]{3,2,1,0:T(8,128)(2,1)}), bf16[8,2,512,1536]{3,2,1,0:T(8,128)(2,1)}, u32[]{:S(2)}, u32[]{:S(2)}) async-start(bf16[8,2,512,1536]{3,2,1,0:T(8,128)(2,1)} %stack.14), calls=%async_computation.2 | async-start | bytes 50331648 | tf_op jit(solution)/shard_map/all_to_all | solution.py:11
  255.8 15.0 %fusion.5 = (f32[32,12,1536]{2,1,0:T(8,128)}, f32[32,12,1536]{2,1,0:T(8,128)}) fusion(bf16[2,32,12,1536]{3,0,2,1:T(2,128)(2,1)S(1)} %all-to-all-done.1), kind=kLoop, calls=%fused_computation.16 | loop fusion | flops 1179648 | bytes 7077888 | tf_op jit(solution)/shard_map/convert_element_type | solution.py:37
  270.8 3.6 reshape.189
  274.3 3.6 reshape.190
  277.9 32.9 %slice_reduce_fusion.1 = (bf16[32,12,4096]{2,1,0:T(8,128)(2,1)}, bf16[32,12,4096]{2,1,0:T(8,128)(2,1)}) fusion(bf16[2,32,12,4096]{3,0,2,1:T(2,128)(2,1)} %all_to_all.15), kind=kLoop, calls=%fused_computation.3 | loop fusion | bytes 12582912 | tf_op jit(solution)/shard_map/slice | solution.py:86
  310.8 5.6 squeeze.26
  316.4 5.6 squeeze.30
  322.0 3.0 convolution_convert_fusion.3
  325.0 0.9 convolution_convert_fusion.1
  325.9 202.4 %all-to-all-done.2 = bf16[8,2,512,1536]{3,2,1,0:T(8,128)(2,1)} async-done(((bf16[8,2,512,1536]{3,2,1,0:T(8,128)(2,1)}), bf16[8,2,512,1536]{3,2,1,0:T(8,128)(2,1)}, u32[]{:S(2)}, u32[]{:S(2)}) %all-to-all-start.2) | async-done | bytes 25165856 | tf_op jit(solution)/shard_map/all_to_all | solution.py:11
  528.3 13.8 %fusion.33 = (bf16[1,8,512,1536]{3,2,0,1:T(8,128)(2,1)S(1)}, bf16[1,8,512,1536]{3,2,0,1:T(8,128)(2,1)}) fusion(bf16[2,8,512,1536]{3,2,0,1:T(8,128)(2,1)} %bitcast.1), kind=kLoop, calls=%fused_computation.71 | loop fusion | bytes 50331648 | tf_op jit(solution)/shard_map/slice | solution.py:93
  542.1 5.1 fusion.34
  547.2 1.1 multiply_convert_fusion.1
  548.3 3.0 fusion.1
  551.6 9.1 %fusion.35 = f32[384,1536]{1,0:T(8,128)S(1)} fusion(bf16[384,4096]{1,0:T(8,128)(2,1)} %squeeze.30, bf16[4096,1536]{1,0:T(8,128)(2,1)} %bitcast.64), kind=kOutput, calls=%fused_computation.73 | convolution fusion | flops 4831838208 | bytes 18087936 | tf_op jit(solution)/shard_map/dot_general | solution.py:22
  560.7 1.1 multiply_convert_fusion
  561.8 3.1 fusion
  566.7 78.7 %all-reduce.3.cloned.1.call-done = (f32[2,4096,16]{1,2,0:T(8,128)}, f32[2,16,1536]{2,1,0:T(8,128)}) async-done(((f32[2,4096,16]{1,2,0:T(8,128)}, f32[2,16,1536]{2,1,0:T(8,128)}), (f32[2,4096,16]{1,2,0:T(8,128)}, f32[2,16,1536]{2,1,0:T(8,128)})) %all-reduce.3.cloned.1.call-update) | async-done | bytes 720912 | tf_op jit(solution)/shard_map/psum | solution.py:111
  645.5 1.9 copy.29
  647.3 1.6 copy.30
  (39 shorter events, 5.0 us)
Async XLA Ops:
  7.2 31.3 %copy-start = (bf16[128,4096]{1,0:T(8,128)(2,1)S(1)}, bf16[128,4096]{1,0:T(8,128)(2,1)}, u32[]{:S(2)}) copy-start(bf16[128,4096]{1,0:T(8,128)(2,1)} %param.6) | copy-start | bytes 3145732
  26.7 64.6 %all-to-all-start.1 = ((bf16[2,32,12,1536]{3,0,2,1:T(2,128)(2,1)}), bf16[2,32,12,1536]{3,0,2,1:T(2,128)(2,1)S(1)}, u32[]{:S(2)}, u32[]{:S(2)}) async-start(bf16[2,32,12,1536]{3,0,2,1:T(2,128)(2,1)} %copy.20), calls=%async_computation.1 | async-start | bytes 4718592 | tf_op jit(solution)/shard_map/all_to_all | solution.py:81
  91.4 117.3 %copy-start.4 = (bf16[2,512,1536]{2,1,0:T(8,128)(2,1)S(1)}, bf16[2,512,1536]{2,1,0:T(8,128)(2,1)}, u32[]{:S(2)}) copy-start(bf16[2,512,1536]{2,1,0:T(8,128)(2,1)} %param.9) | copy-start | bytes 9437188
  217.3 311.0 %all-to-all-start.2 = ((bf16[8,2,512,1536]{3,2,1,0:T(8,128)(2,1)}), bf16[8,2,512,1536]{3,2,1,0:T(8,128)(2,1)}, u32[]{:S(2)}, u32[]{:S(2)}) async-start(bf16[8,2,512,1536]{3,2,1,0:T(8,128)(2,1)} %stack.14), calls=%async_computation.2 | async-start | bytes 50331648 | tf_op jit(solution)/shard_map/all_to_all | solution.py:11
  255.6 389.9 %all-reduce.3.cloned.1.call-start = ((), (), s32[]{:S(2)}) async-start(), calls=%async_computation.3 | async-start | bytes 1441792 | tf_op jit(solution)/shard_map/psum | solution.py:111
  316.4 5.6 copy-start.7
  322.0 3.0 copy-start.2
  528.3 13.8 %copy-start.3 = (bf16[384,4096]{1,0:T(8,128)(2,1)S(1)}, bf16[384,4096]{1,0:T(8,128)(2,1)}, u32[]{:S(2)}) copy-start(bf16[384,4096]{1,0:T(8,128)(2,1)} %squeeze.26) | copy-start | bytes 9437188
  542.1 5.1 copy-start.6
  542.1 5.1 copy-start.8
  551.6 9.1 %copy-start.5 = (f32[384,1536]{1,0:T(8,128)S(1)}, f32[384,1536]{1,0:T(8,128)}, u32[]{:S(2)}) copy-start(f32[384,1536]{1,0:T(8,128)} %reshape.190) | copy-start | bytes 7077892
  561.8 87.1 %copy-start.1 = (bf16[128,4096]{1,0:T(8,128)(2,1)S(1)}, bf16[128,4096]{1,0:T(8,128)(2,1)}, u32[]{:S(2)}) copy-start(bf16[128,4096]{1,0:T(8,128)(2,1)} %param.6) | copy-start | bytes 3145732
Sparse Core Ops, SparseCore 0:
  566.9 78.5 all-reduce.2
